TPU v7x, 32 devices: a whole 2x2x4 slice. The times are simulated.
32 devices in a mesh: section: 4 (over y, core), fsdp: 8 (over z, x).
Axes of the slice: x: 2, y: 2, z: 4, core: 2. Of those that a mesh axis runs over, the one named last changes fastest.
Arguments:
- old_pieces: bfloat16 [4, 2, 16384, 1024], P('section', None, 'fsdp'), may hold values from -0.0625 to 0.0625
- section_inputs: bfloat16 [4, 4096, 8192], P('section', 'fsdp'), may hold values from -6 to 6
- old_section_of: int32 [8], replicated, may hold values from 0 to 3, as said below
- new_section_of: int32 [8], replicated, may hold values from 0 to 7, as said below
- old_order: int32 [8, 2], replicated, may hold values from 0 to 1, each once within a row
- new_order: int32 [8, 2], replicated, may hold values from 0 to 1, each once within a row
Outputs:
- new_shards: bfloat16 [4, 32768, 1024], P('section', 'fsdp')
- kv_out: bfloat16 [4, 4096, 2048], P('section', 'fsdp')
Inputs may be any that keep to these rules, and one draw needn't show every extreme that they name: `old_section_of`: each old section holds exactly two layers. Each new section holds exactly one layer; the two layers of one old section have different values of new_section_of // 2.
All inputs are finite; a program needn't handle non-finite values.
Results may differ from a plain program's by a relative error of at most 0.001.
Values may be sent and summed in bfloat16 or wider, within the bound.
A program may use at most 192 MiB of HBM per device.

v0:
```python
import functools
import math

import jax
import jax.numpy as jnp
import numpy as np
from jax import lax
from jax.experimental import pallas as pl
from jax.experimental.pallas import tpu as pltpu
from jax.sharding import PartitionSpec as P


HEAD_DIM = 128


CHUNK = HEAD_DIM
MESH = pl.DeviceIdType.MESH
CROSS_LAG = 11
RETURN_LAG = 6
CHUNK_STEPS = 3
PIECES_PER_STEP = 3


def chain_kernel(
    block_rows, piece_rows,
    old_ref, tok_ref, old_sec, new_sec, old_ord, new_ord, freq_ref,
    shard_ref, kv_ref, relay_ref, middle_ref,
    oldv, send, keep, recv, held, forv, cross, tokv, cos_t, sin_t,
    relay_w, middle_w, sums, sumr, acc, kvst, shst,
    old_sem, sec_send_sem, sec_recv_sem, x_send_sem, x_recv_sem, own_send_sem, relay_sem,
    middle_sem, fwd_send_sem, ret_send_sem, cross_sem, tok_sem, piece_send_sem, piece_recv_sem,
    weight_sem, sum_send_sem, sum_recv_sem, kv_sem, shard_sem,
):
    rows = old_ref.shape[2]
    kv_width = old_ref.shape[3]
    tok_rows = tok_ref.shape[1]
    half_width = tok_ref.shape[2] // 2
    chunks = kv_width // CHUNK
    blocks = rows // block_rows
    steps = chunks * blocks
    pieces = tok_rows // piece_rows
    layers = old_sec.shape[0]

    sec = lax.axis_index("section")
    member = lax.axis_index("fsdp")
    z, x = member // 2, member % 2
    upper = z // 2
    inner = (z == 1) | (z == 2)
    outer = (z == 0) | (z == 3)
    side = z % 2
    across = {"fsdp": (3 - z) * 2 + x}
    beside = {"fsdp": (z + 1 - 2 * side) * 2 + x}
    partner = {"fsdp": z * 2 + 1 - x}

    def section_at(offset):
        flip_core, flip_y = offset % 2, offset // 2
        core, y = sec % 2, sec // 2
        core = 1 - core if flip_core else core
        y = 1 - y if flip_y else y
        return y * 2 + core

    barrier = pltpu.get_barrier_semaphore()
    for offset in (1, 2, 3):
        pl.semaphore_signal(
            barrier, inc=1, device_id={"section": section_at(offset)}, device_id_type=MESH
        )
    pl.semaphore_signal(barrier, inc=1, device_id=partner, device_id_type=MESH)
    pl.semaphore_signal(barrier, inc=1, device_id=beside, device_id_type=MESH)

    @pl.when(inner)
    def _():
        pl.semaphore_signal(barrier, inc=1, device_id=across, device_id_type=MESH)

    def old_load(t):
        j, b = t // blocks, t % blocks
        return pltpu.make_async_copy(
            old_ref.at[0, :, pl.ds(b * block_rows, block_rows), pl.ds(j * CHUNK, CHUNK)],
            oldv.at[t % 2],
            old_sem.at[t % 2],
        )

    def tok_load(which):
        column = (side if which == 0 else 1 - side) * half_width
        return pltpu.make_async_copy(
            tok_ref.at[0, :, pl.ds(column, half_width)], tokv.at[which], tok_sem.at[which]
        )

    old_load(0).start()
    old_load(1).start()
    tok_load(0).start()
    tok_load(1).start()

    target_low = jnp.int32(0)
    own_from, foreign_from = jnp.int32(0), jnp.int32(0)
    old_first, new_first = jnp.int32(0), jnp.int32(0)
    seen = jnp.int32(0)
    for layer in range(layers):
        here = old_sec[layer] == sec
        place = new_sec[layer]
        target_low = jnp.where(here & (seen == 0), place // 2, target_low)
        seen = jnp.where(here, 1, seen)
        own_from = jnp.where(place == 2 * sec + x, old_sec[layer], own_from)
        foreign_from = jnp.where(place == 2 * sec + 1 - x, old_sec[layer], foreign_from)
        old_first = jnp.where(place == 2 * sec + x, old_ord[layer, 0], old_first)
        new_first = jnp.where(place == 2 * sec + x, new_ord[layer, 0], new_first)
    flipped = old_first != new_first
    own_is_key = old_first == upper

    @pl.when(inner)
    def _():
        pl.semaphore_wait(barrier, 6)

    @pl.when(outer)
    def _():
        pl.semaphore_wait(barrier, 5)

    def place_of(t):
        return t // blocks, pl.ds(pl.multiple_of((t % blocks) * block_rows, block_rows), block_rows)

    def sec_copy(t, offset):
        return pltpu.make_async_remote_copy(
            src_ref=send.at[t % 2, offset - 1],
            dst_ref=recv.at[t, offset - 1],
            send_sem=sec_send_sem.at[t % 2, offset - 1],
            recv_sem=sec_recv_sem.at[t, offset - 1],
            device_id={"section": section_at(offset)},
            device_id_type=MESH,
        )

    def x_copy(t):
        j, at = place_of(t)
        return pltpu.make_async_remote_copy(
            src_ref=forv.at[t % 2],
            dst_ref=held.at[j, x, at],
            send_sem=x_send_sem.at[t % 2],
            recv_sem=x_recv_sem.at[t],
            device_id=partner,
            device_id_type=MESH,
        )

    def own_copy(t, to_middle):
        j, at = place_of(t)
        return pltpu.make_async_remote_copy(
            src_ref=held.at[j, :, at],
            dst_ref=(middle_ref if to_middle else relay_ref).at[j, :, at],
            send_sem=own_send_sem.at[t],
            recv_sem=(middle_sem if to_middle else relay_sem).at[t],
            device_id=across if to_middle else beside,
            device_id_type=MESH,
        )

    def cross_copy(t, forward):
        j, at = place_of(t)
        return pltpu.make_async_remote_copy(
            src_ref=(relay_ref if forward else middle_ref).at[j, :, at],
            dst_ref=cross.at[j, :, at],
            send_sem=(fwd_send_sem if forward else ret_send_sem).at[t],
            recv_sem=cross_sem.at[t],
            device_id=across if forward else beside,
            device_id_type=MESH,
        )

    def piece_copy(p):
        at = pl.ds(pl.multiple_of(p * piece_rows, piece_rows), piece_rows)
        column = (1 - side) * half_width
        return pltpu.make_async_remote_copy(
            src_ref=tok_ref.at[0, at, pl.ds(column, half_width)],
            dst_ref=tokv.at[2, at],
            send_sem=piece_send_sem.at[p],
            recv_sem=piece_recv_sem.at[p],
            device_id=beside,
            device_id_type=MESH,
        )

    def sum_copy(j, which):
        return pltpu.make_async_remote_copy(
            src_ref=sums.at[j % 2, which],
            dst_ref=sumr.at[j, which],
            send_sem=sum_send_sem.at[j % 2, which],
            recv_sem=sum_recv_sem.at[j, which],
            device_id=beside,
            device_id_type=MESH,
        )

    def weight_load(j, which):
        return pltpu.make_async_copy(
            (middle_ref if which else relay_ref).at[j],
            middle_w if which else relay_w,
            weight_sem.at[which],
        )

    def kv_store(j, which):
        return pltpu.make_async_copy(
            kvst.at[j % 2, which],
            kv_ref.at[0, :, pl.ds(which * kv_width + j * CHUNK, CHUNK)],
            kv_sem.at[j % 2, which],
        )

    def shard_store(j):
        return pltpu.make_async_copy(
            shst.at[j % 2],
            shard_ref.at[:, :, pl.ds(j * CHUNK, CHUNK)],
            shard_sem.at[j % 2],
        )

    tile = min(256, tok_rows)
    tiles = tok_rows // tile

    def product(which, weights, at):
        near = jnp.dot(
            tokv[which, at, pl.ds(0, rows)], weights[0], preferred_element_type=jnp.float32
        )
        far = jnp.dot(
            tokv[which, at, pl.ds(rows, rows)], weights[1], preferred_element_type=jnp.float32
        )
        return near + far

    def each_tile(body):
        def run(i, carry):
            body(pl.ds(pl.multiple_of(i * tile, tile), tile))
            return carry

        lax.fori_loop(0, tiles, run, 0)

    def angles():
        part = min(64, tok_rows)

        def run(i, carry):
            at = pl.ds(pl.multiple_of(i * part, part), part)
            base = z * tok_rows + i * part
            position = base + lax.broadcasted_iota(jnp.int32, (part, CHUNK), 0)
            angle = position.astype(jnp.float32) * freq_ref[...]
            lane = lax.broadcasted_iota(jnp.int32, (part, CHUNK), 1)
            cos_t[at] = jnp.cos(angle)
            sine = jnp.sin(angle)
            sin_t[at] = jnp.where(lane < CHUNK // 2, -sine, sine)
            return carry

        lax.fori_loop(0, tok_rows // part, run, 0)

    first_compute = steps + CROSS_LAG - CHUNK_STEPS * (chunks - 1)

    def compute_own(j):
        @pl.when(j == 0)
        def _():
            tok_load(0).wait()
            tok_load(1).wait()

            @pl.when(inner)
            def _():
                def wait_piece(p, carry):
                    piece_copy(p).wait_recv()
                    return carry

                lax.fori_loop(0, pieces, wait_piece, 0)

        @pl.when(inner)
        def _():
            @pl.when(j >= 2)
            def _():
                sum_copy(j - 2, 0).wait_send()

            def foreign(at):
                sums[j % 2, 0, at] = product(2, held.at[j], at)

            each_tile(foreign)
            sum_copy(j, 0).start()
            weight_load(j, 0).wait()
            weight_load(j, 1).wait()

            def both(at):
                acc[0, at] = product(0, held.at[j], at) + product(1, relay_w, at)
                acc[1, at] = product(1, middle_w, at)

            each_tile(both)

        @pl.when(outer)
        def _():
            def mine(at):
                acc[0, at] = product(0, held.at[j], at)

            each_tile(mine)

    def compute_cross(j):
        for b in range(blocks):
            cross_copy(j * blocks + b, True).wait_recv()

        @pl.when(inner)
        def _():
            @pl.when(j >= 2)
            def _():
                sum_copy(j - 2, 1).wait_send()

            def foreign(at):
                sums[j % 2, 1, at] = product(2, cross.at[j], at)

            each_tile(foreign)
            sum_copy(j, 1).start()

            def mine(at):
                acc[1, at] = acc[1, at] + product(0, cross.at[j], at)

            each_tile(mine)

        @pl.when(outer)
        def _():
            def mine(at):
                acc[1, at] = product(0, cross.at[j], at)

            each_tile(mine)

        @pl.when(j >= 2)
        def _():
            shard_store(j - 2).wait()
            kv_store(j - 2, 0).wait()
            kv_store(j - 2, 1).wait()

        shst[j % 2] = jnp.where(flipped, cross[j], held[j])
        shard_store(j).start()

        @pl.when(outer)
        def _():
            for which in range(2):
                sum_copy(j, which).wait_recv()
                acc[which] = acc[which] + sumr[j, which]

        first, second = acc[0], acc[1]
        keys = jnp.where(own_is_key, first, second)
        values = jnp.where(own_is_key, second, first)
        turned = keys * cos_t[...] + pltpu.roll(keys, CHUNK // 2, 1) * sin_t[...]
        kvst[j % 2, 0] = turned.astype(kvst.dtype)
        kvst[j % 2, 1] = values.astype(kvst.dtype)
        kv_store(j, 0).start()
        kv_store(j, 1).start()

    def step(tau, carry):
        @pl.when(tau < steps)
        def _():
            t = tau
            old_load(t).wait()

            @pl.when(t >= 2)
            def _():
                for offset in (1, 2, 3):
                    sec_copy(t - 2, offset).wait_send()

            low, high = oldv[t % 2, 0], oldv[t % 2, 1]
            for offset in (2, 3, 1):
                send[t % 2, offset - 1] = jnp.where(target_low == section_at(offset), low, high)
            keep[t % 4] = jnp.where(target_low == sec, low, high)
            for offset in (2, 3, 1):
                sec_copy(t, offset).start()

            @pl.when(t + 2 < steps)
            def _():
                old_load(t + 2).start()

        @pl.when(outer)
        def _():
            for k in range(PIECES_PER_STEP):
                p = tau * PIECES_PER_STEP + k

                @pl.when(p < pieces)
                def _():
                    piece_copy(p).start()

        @pl.when((tau >= 2) & (tau < steps + 2))
        def _():
            t = tau - 2
            for offset in (1, 2, 3):
                sec_copy(t, offset).wait_recv()

            @pl.when(t >= 2)
            def _():
                x_copy(t - 2).wait_send()

            j, at = place_of(t)
            own, foreign = keep[t % 4], keep[t % 4]
            for offset in (1, 2, 3):
                arrived = recv[t, offset - 1]
                own = jnp.where(own_from == section_at(offset), arrived, own)
                foreign = jnp.where(foreign_from == section_at(offset), arrived, foreign)
            forv[t % 2] = foreign
            held[j, x, at] = own
            x_copy(t).start()

        @pl.when((tau >= 3) & (tau < steps + 3))
        def _():
            t = tau - 3
            x_copy(t).wait_recv()

            @pl.when(outer)
            def _():
                own_copy(t, False).start()

            @pl.when(inner)
            def _():
                own_copy(t, True).start()

        @pl.when(inner & (tau >= RETURN_LAG) & (tau < steps + RETURN_LAG))
        def _():
            t = tau - RETURN_LAG
            own_copy(t, True).wait_recv()
            cross_copy(t, False).start()

        @pl.when(inner & (tau >= CROSS_LAG) & (tau < steps + CROSS_LAG))
        def _():
            t = tau - CROSS_LAG
            own_copy(t, False).wait_recv()
            cross_copy(t, True).start()

        @pl.when(tau == 4)
        def _():
            angles()

        since = tau - first_compute + 1
        j = since // CHUNK_STEPS
        phase = since % CHUNK_STEPS
        live = (since >= 0) & (j < chunks)

        @pl.when(inner & live & (phase == 0))
        def _():
            weight_load(j, 0).start()
            weight_load(j, 1).start()

        @pl.when(live & (phase == 1))
        def _():
            compute_own(j)

        @pl.when(live & (phase == 2))
        def _():
            compute_cross(j)

        return carry

    lax.fori_loop(0, steps + CROSS_LAG + 2, step, 0)

    for t in (steps - 2, steps - 1):
        for offset in (1, 2, 3):
            sec_copy(t, offset).wait_send()
        x_copy(t).wait_send()

    def drain(t, carry):
        @pl.when(outer)
        def _():
            own_copy(t, False).wait_send()

        @pl.when(inner)
        def _():
            own_copy(t, True).wait_send()
            cross_copy(t, False).wait_send()
            cross_copy(t, True).wait_send()

        return carry

    lax.fori_loop(0, steps, drain, 0)

    @pl.when(outer)
    def _():
        def drain_piece(p, carry):
            piece_copy(p).wait_send()
            return carry

        lax.fori_loop(0, pieces, drain_piece, 0)

    for j in (chunks - 2, chunks - 1):
        @pl.when(inner)
        def _():
            for which in range(2):
                sum_copy(j, which).wait_send()

        for which in range(2):
            kv_store(j, which).wait()
        shard_store(j).wait()


def per_device_chain(old_pieces, section_inputs, old_sec, new_sec, old_ord, new_ord):
    _, layers_held, rows, kv_width = old_pieces.shape
    _, tok_rows, width = section_inputs.shape
    chunks = kv_width // CHUNK
    block_rows = rows // 4
    steps = chunks * 4
    piece_rows = tok_rows // 32
    pieces = tok_rows // piece_rows
    half_dim = HEAD_DIM // 2
    index = np.arange(half_dim, dtype=np.float32)
    factor = np.float32(-2.0 * math.log(500000.0) / HEAD_DIM)
    freq = np.exp((index * factor).astype(np.float64)).astype(np.float32)
    freq = jnp.asarray(np.concatenate([freq, freq])[None])
    kind = old_pieces.dtype
    dma = pltpu.SemaphoreType.DMA
    hbm = pl.BlockSpec(memory_space=pltpu.HBM)
    smem = pl.BlockSpec(memory_space=pltpu.SMEM)
    shard, kv, _, _ = pl.pallas_call(
        functools.partial(chain_kernel, block_rows, piece_rows),
        out_shape=(
            jax.ShapeDtypeStruct((2, rows, kv_width), kind),
            jax.ShapeDtypeStruct((1, tok_rows, 2 * kv_width), kind),
            jax.ShapeDtypeStruct((chunks, 2, rows, CHUNK), kind),
            jax.ShapeDtypeStruct((chunks, 2, rows, CHUNK), kind),
        ),
        in_specs=[hbm, hbm, smem, smem, smem, smem, pl.BlockSpec(memory_space=pltpu.VMEM)],
        out_specs=(hbm, hbm, hbm, hbm),
        scratch_shapes=[
            pltpu.VMEM((2, layers_held, block_rows, CHUNK), kind),
            pltpu.VMEM((2, 3, block_rows, CHUNK), kind),
            pltpu.VMEM((4, block_rows, CHUNK), kind),
            pltpu.VMEM((steps, 3, block_rows, CHUNK), kind),
            pltpu.VMEM((chunks, 2, rows, CHUNK), kind),
            pltpu.VMEM((2, block_rows, CHUNK), kind),
            pltpu.VMEM((chunks, 2, rows, CHUNK), kind),
            pltpu.VMEM((3, tok_rows, width // 2), kind),
            pltpu.VMEM((tok_rows, CHUNK), jnp.float32),
            pltpu.VMEM((tok_rows, CHUNK), jnp.float32),
            pltpu.VMEM((2, rows, CHUNK), kind),
            pltpu.VMEM((2, rows, CHUNK), kind),
            pltpu.VMEM((2, 2, tok_rows, CHUNK), jnp.float32),
            pltpu.VMEM((chunks, 2, tok_rows, CHUNK), jnp.float32),
            pltpu.VMEM((2, tok_rows, CHUNK), jnp.float32),
            pltpu.VMEM((2, 2, tok_rows, CHUNK), kind),
            pltpu.VMEM((2, 2, rows, CHUNK), kind),
            dma((2,)),
            dma((2, 3)),
            dma((steps, 3)),
            dma((2,)),
            dma((steps,)),
            dma((steps,)),
            dma((steps,)),
            dma((steps,)),
            dma((steps,)),
            dma((steps,)),
            dma((steps,)),
            dma((2,)),
            dma((pieces,)),
            dma((pieces,)),
            dma((2,)),
            dma((2, 2)),
            dma((chunks, 2)),
            dma((2, 2)),
            dma((2,)),
        ],
        compiler_params=pltpu.CompilerParams(
            collective_id=0, has_side_effects=True, vmem_limit_bytes=60 * 2**20
        ),
    )(old_pieces, section_inputs, old_sec, new_sec, old_ord, new_ord, freq)
    return shard.reshape(1, 2 * rows, kv_width), kv


def from_partner(block, axis, stride):
    count = lax.axis_size(axis)
    route = []
    for low in range(count):
        high = low | 1 << stride
        if high != low and high < count:
            route += [(low, high), (high, low)]
    return lax.ppermute(block, axis, route)


def from_offset(block, axis, offset):
    count = lax.axis_size(axis)
    return lax.ppermute(block, axis, [(i, i ^ offset) for i in range(count)])


def rotate_keys(values, positions):
    tok_rows = values.shape[0]
    heads = values.reshape(tok_rows, -1, HEAD_DIM)
    half_dim = HEAD_DIM // 2
    freq_index = jnp.arange(half_dim, dtype=jnp.float32)
    inverse_freq = jnp.exp(freq_index * (-2.0 * math.log(500000.0) / HEAD_DIM))
    angles = positions.astype(jnp.float32)[:, None] * inverse_freq[None, :]
    cosine = jnp.cos(angles)[:, None, :]
    sine = jnp.sin(angles)[:, None, :]
    lower = heads[..., :half_dim]
    upper = heads[..., half_dim:]
    turned = jnp.concatenate(
        [lower * cosine - upper * sine, upper * cosine + lower * sine], axis=-1
    )
    return turned.reshape(tok_rows, -1)


def pick_entry(table, index_value):
    positions = jnp.arange(table.shape[0], dtype=jnp.int32)
    return jnp.sum(jnp.where(positions == index_value, table, 0))


def pick_row(table, index_value):
    positions = jnp.arange(table.shape[0], dtype=jnp.int32)[:, None]
    return jnp.sum(jnp.where(positions == index_value, table, 0), axis=0)


def chunk_columns(kv_width):
    heads = kv_width // HEAD_DIM
    edge = [1, 1] if heads >= 4 else []
    middle = heads - len(edge)
    sizes = [2] * (middle // 2) + [1] * (middle % 2) + edge
    starts = [sum(sizes[:i]) for i in range(len(sizes))]
    return [(s * HEAD_DIM, n * HEAD_DIM) for s, n in zip(starts, sizes)]


def per_device(old_pieces, section_inputs, old_section_of, new_section_of, old_order, new_order):
    section_count = lax.axis_size("section")
    member_count = lax.axis_size("fsdp")
    digit_count = member_count.bit_length() - 1
    row_index = lax.axis_index("section")
    member = lax.axis_index("fsdp")
    parity = member % 2
    layer_total = old_section_of.shape[0]
    layer_ids = jnp.arange(layer_total, dtype=jnp.int32)
    in_row = old_section_of == row_index
    layer_low = jnp.min(jnp.where(in_row, layer_ids, layer_total))
    layer_high = jnp.max(jnp.where(in_row, layer_ids, -1))
    target_low = pick_entry(new_section_of, layer_low) // 2
    layer_own = jnp.sum(jnp.where(new_section_of == 2 * row_index + parity, layer_ids, 0))
    layer_foreign = jnp.sum(jnp.where(new_section_of == 2 * row_index + 1 - parity, layer_ids, 0))
    source_own = pick_entry(old_section_of, layer_own)
    source_foreign = pick_entry(old_section_of, layer_foreign)
    pieces = old_pieces[0]
    tokens = section_inputs[0]
    tok_rows, _ = tokens.shape
    shard_rows, kv_width = 2 * pieces.shape[1], pieces.shape[2]
    own_bits = {digit: member // 2**digit % 2 for digit in range(1, digit_count)}
    own_old = pick_row(old_order, layer_own)
    own_new = pick_row(new_order, layer_own)
    flipped = own_old[0] != own_new[0]
    group_digits = digit_count - 1
    low_count = group_digits // 2
    high_digits = list(range(low_count + 1, digit_count))
    low_digits = list(range(1, low_count + 1))
    top_bit = own_bits[digit_count - 1]

    def to_groups(low, high):
        sources = []
        for offset in range(section_count):
            chosen = jnp.where(target_low == row_index ^ offset, low, high)
            if offset:
                chosen = from_offset(chosen, "section", offset)
            sources.append(chosen)
        (own_from, foreign_from, here, side), sources = lax.optimization_barrier(
            ((source_own, source_foreign, row_index, parity), sources)
        )
        own, foreign = sources[0], sources[0]
        for offset in range(1, section_count):
            own = jnp.where(own_from == here ^ offset, sources[offset], own)
            foreign = jnp.where(foreign_from == here ^ offset, sources[offset], foreign)
        partner = from_partner(foreign, "fsdp", 0)
        lower = jnp.where(side == 0, own, partner)
        upper = jnp.where(side == 0, partner, own)
        return jnp.concatenate([lower, upper], axis=-2)

    def gather_high(block):
        blocks = [block]
        for digit in high_digits:
            blocks += [from_partner(held, "fsdp", digit) for held in blocks]
        return blocks

    block_digits = high_digits[:-1]
    place_digits = block_digits[::-1] + low_digits[::-1]

    def pick_columns(flips):
        column = 0
        for digit in place_digits:
            column = 2 * column + (own_bits[digit] ^ flips[digit])
        return lax.dynamic_slice_in_dim(tokens, column * shard_rows, shard_rows, axis=1)

    row_cuts = 4 if tok_rows % 64 == 0 else 1
    token_blocks = {}
    for number in range(2 ** len(block_digits)):
        flips = {digit: number >> place & 1 for place, digit in enumerate(block_digits)}
        pending = {}
        for want in range(2**low_count):
            low_flips = {digit: want >> place & 1 for place, digit in enumerate(low_digits)}
            pending[want] = pick_columns({**flips, **low_flips})
        for place, digit in enumerate(low_digits):
            moved = dict(pending)
            for want in range(2**low_count):
                if want >> place & 1:
                    cuts = jnp.split(pending[want], row_cuts, axis=0)
                    cuts = [from_partner(cut, "fsdp", digit) for cut in cuts]
                    moved[want] = jnp.concatenate(cuts, axis=0)
            pending = moved
        for want in range(2**low_count):
            token_blocks[want, number] = pending[want]

    def project(blocks):
        sums = []
        for want in reversed(range(2**low_count)):
            for number, block in enumerate(blocks):
                product = jnp.dot(
                    token_blocks[want, number], block, preferred_element_type=jnp.float32
                )
                total = total + product if number else product
            sums.append(total)
        sums = sums[::-1]
        for place in reversed(range(low_count)):
            half = len(sums) // 2
            sums = [
                kept + from_partner(sent, "fsdp", low_digits[place])
                for kept, sent in zip(sums[:half], sums[half:])
            ]
        return sums[0]

    positions = member // 2 * tok_rows + jnp.arange(tok_rows, dtype=jnp.int32)
    shard_parts, key_parts, value_parts = [], [], []
    for number, (start, width) in enumerate(chunk_columns(kv_width)):
        part = lax.slice_in_dim(pieces, start, start + width, axis=2)
        if number == 0:
            crossed = jnp.stack(gather_high(part), axis=1)
            held = to_groups(crossed[0], crossed[1])
            blocks = [held[i] for i in range(held.shape[0])]
        else:
            blocks = gather_high(to_groups(part[0], part[1]))
        half = len(blocks) // 2
        near = project(blocks[:half])
        far = project(blocks[half:])
        shard_parts.append(jnp.where(flipped, blocks[half], blocks[0]))
        keys = jnp.where(own_old[0] == top_bit, near, far)
        values = jnp.where(own_old[1] == top_bit, near, far)
        key_parts.append(rotate_keys(keys, positions).astype(jnp.bfloat16))
        value_parts.append(values.astype(jnp.bfloat16))
    new_shard = jnp.concatenate(shard_parts, axis=1)
    joined = jnp.concatenate(key_parts + value_parts, axis=1)
    return (new_shard[None], joined[None])


def solution(mesh):
    in_specs = (P("section", None, "fsdp", None), P("section", "fsdp", None), P(), P(), P(), P())
    out_specs = (P("section", "fsdp", None), P("section", "fsdp", None))

    if dict(mesh.shape) == {"section": 4, "fsdp": 8}:
        return jax.shard_map(
            per_device_chain, mesh=mesh, in_specs=in_specs, out_specs=out_specs, check_vma=False
        )

    return jax.shard_map(
        per_device, mesh=mesh, in_specs=in_specs, out_specs=out_specs, check_vma=False
    )
```

profile of v0, /device:TPU:0, one launch (start us, length us, event | category | flops | bytes accessed | tf_op | source)
XLA Modules:
  0.0 405.1 jit_solution(3211660356301538753)
XLA Ops:
  0.6 1.3 copy.9.old_ord
  2.0 1.3 copy.10.new_ord
  3.3 392.5 %shard_map.86 = (bf16[2,2048,1024]{2,1,0:T(8,128)(2,1)}, bf16[1,512,2048]{2,1,0:T(8,128)(2,1)}, bf16[8,2,2048,128]{3,2,1,0:T(8,128)(2,1)}, bf16[8,2,2048,128]{3,2,1,0:T(8,128)(2,1)}) custom-call(bf16[1,2,2048,1024]{3,2,1,0:T(8,128)(2,1)} %old_ref.1, bf16[1,512,8192]{2,1,0:T(8,128)(2,1)} %tok_ref.1, s32[8]{0:T(128)} %old_sec.1, s32[8]{0:T(128)} %new_sec.1, ...), custom_call_target="tpu_custom_call" | custom-call | tf_op jit(solution)/shard_map/pallas_call | solution.py:494
  395.8 0.0 copy-start
  395.8 7.9 %copy.13 = bf16[1,4096,1024]{2,1,0:T(8,128)(2,1)} copy(bf16[1,4096,1024]{2,1,0:T(8,128)(2,1)} %bitcast.1) | data formatting | bytes 16777216
  403.7 0.0 copy-done
  403.8 1.3 copy.14
Async XLA Ops:
  395.8 7.9 %copy-start = (bf16[1,512,2048]{2,1,0:T(8,128)(2,1)S(1)}, bf16[1,512,2048]{2,1,0:T(8,128)(2,1)}, u32[]{:S(2)}) copy-start(bf16[1,512,2048]{2,1,0:T(8,128)(2,1)} %get-tuple-element.9) | copy-start | bytes 6291460
where the time goes:
time: 405 us
  Pallas kernels  393 us (97%)
  local copies, waits for them, and re-layouts  11.9 us (3%)
    pallas_call x1, Pallas kernels, per_device_chain(): pl.pallas_call(functools.partial(chain_kernel, block_rows, piece_rows), o...  393 us
    unnamed x6, local copies, waits for them, and re-layouts  11.9 us

commit v1 on v0

--- a/solution.py
+++ b/solution.py
@@ -26,10 +26,10 @@
     old_ref, tok_ref, old_sec, new_sec, old_ord, new_ord, freq_ref,
     shard_ref, kv_ref, relay_ref, middle_ref,
     oldv, send, keep, recv, held, forv, cross, tokv, cos_t, sin_t,
-    relay_w, middle_w, sums, sumr, acc, kvst, shst,
+    relay_w, middle_w, sums, sumr, acc,
     old_sem, sec_send_sem, sec_recv_sem, x_send_sem, x_recv_sem, own_send_sem, relay_sem,
     middle_sem, fwd_send_sem, ret_send_sem, cross_sem, tok_sem, piece_send_sem, piece_recv_sem,
-    weight_sem, sum_send_sem, sum_recv_sem, kv_sem, shard_sem,
+    weight_sem, sum_send_sem, sum_recv_sem,
 ):
     rows = old_ref.shape[2]
     kv_width = old_ref.shape[3]
@@ -101,8 +101,8 @@
         seen = jnp.where(here, 1, seen)
         own_from = jnp.where(place == 2 * sec + x, old_sec[layer], own_from)
         foreign_from = jnp.where(place == 2 * sec + 1 - x, old_sec[layer], foreign_from)
-        old_first = jnp.where(place == 2 * sec + x, old_ord[layer, 0], old_first)
-        new_first = jnp.where(place == 2 * sec + x, new_ord[layer, 0], new_first)
+        old_first = jnp.where(place == 2 * sec + x, old_ord[0, layer], old_first)
+        new_first = jnp.where(place == 2 * sec + x, new_ord[0, layer], new_first)
     flipped = old_first != new_first
     own_is_key = old_first == upper
 
@@ -189,20 +189,6 @@
             weight_sem.at[which],
         )
 
-    def kv_store(j, which):
-        return pltpu.make_async_copy(
-            kvst.at[j % 2, which],
-            kv_ref.at[0, :, pl.ds(which * kv_width + j * CHUNK, CHUNK)],
-            kv_sem.at[j % 2, which],
-        )
-
-    def shard_store(j):
-        return pltpu.make_async_copy(
-            shst.at[j % 2],
-            shard_ref.at[:, :, pl.ds(j * CHUNK, CHUNK)],
-            shard_sem.at[j % 2],
-        )
-
     tile = min(256, tok_rows)
     tiles = tok_rows // tile
 
@@ -309,14 +295,7 @@
 
             each_tile(mine)
 
-        @pl.when(j >= 2)
-        def _():
-            shard_store(j - 2).wait()
-            kv_store(j - 2, 0).wait()
-            kv_store(j - 2, 1).wait()
-
-        shst[j % 2] = jnp.where(flipped, cross[j], held[j])
-        shard_store(j).start()
+        shard_ref[j] = jnp.where(flipped, cross[j], held[j])
 
         @pl.when(outer)
         def _():
@@ -328,10 +307,8 @@
         keys = jnp.where(own_is_key, first, second)
         values = jnp.where(own_is_key, second, first)
         turned = keys * cos_t[...] + pltpu.roll(keys, CHUNK // 2, 1) * sin_t[...]
-        kvst[j % 2, 0] = turned.astype(kvst.dtype)
-        kvst[j % 2, 1] = values.astype(kvst.dtype)
-        kv_store(j, 0).start()
-        kv_store(j, 1).start()
+        kv_ref[0, j] = turned.astype(kv_ref.dtype)
+        kv_ref[1, j] = values.astype(kv_ref.dtype)
 
     def step(tau, carry):
         @pl.when(tau < steps)
@@ -469,9 +446,27 @@
             for which in range(2):
                 sum_copy(j, which).wait_send()
 
+
+def store_kernel(held_shard, held_kv, shard_ref, kv_ref, shard_sem, kv_sem):
+    chunks = held_shard.shape[0]
+    kv_width = shard_ref.shape[2]
+    copies = []
+    for j in range(chunks):
+        at = pl.ds(j * CHUNK, CHUNK)
+        copies.append(
+            pltpu.make_async_copy(held_shard.at[j], shard_ref.at[:, :, at], shard_sem.at[j])
+        )
         for which in range(2):
-            kv_store(j, which).wait()
-        shard_store(j).wait()
+            at = pl.ds(which * kv_width + j * CHUNK, CHUNK)
+            copies.append(
+                pltpu.make_async_copy(
+                    held_kv.at[which, j], kv_ref.at[0, :, at], kv_sem.at[which, j]
+                )
+            )
+    for copy in copies:
+        copy.start()
+    for copy in copies:
+        copy.wait()
 
 
 def per_device_chain(old_pieces, section_inputs, old_sec, new_sec, old_ord, new_ord):
@@ -491,16 +486,17 @@
     dma = pltpu.SemaphoreType.DMA
     hbm = pl.BlockSpec(memory_space=pltpu.HBM)
     smem = pl.BlockSpec(memory_space=pltpu.SMEM)
-    shard, kv, _, _ = pl.pallas_call(
+    vmem = pl.BlockSpec(memory_space=pltpu.VMEM)
+    held_shard, held_kv, _, _ = pl.pallas_call(
         functools.partial(chain_kernel, block_rows, piece_rows),
         out_shape=(
-            jax.ShapeDtypeStruct((2, rows, kv_width), kind),
-            jax.ShapeDtypeStruct((1, tok_rows, 2 * kv_width), kind),
+            pltpu.VMEM((chunks, 2, rows, CHUNK), kind),
+            pltpu.VMEM((2, chunks, tok_rows, CHUNK), kind),
             jax.ShapeDtypeStruct((chunks, 2, rows, CHUNK), kind),
             jax.ShapeDtypeStruct((chunks, 2, rows, CHUNK), kind),
         ),
-        in_specs=[hbm, hbm, smem, smem, smem, smem, pl.BlockSpec(memory_space=pltpu.VMEM)],
-        out_specs=(hbm, hbm, hbm, hbm),
+        in_specs=[hbm, hbm, smem, smem, smem, smem, vmem],
+        out_specs=(vmem, vmem, hbm, hbm),
         scratch_shapes=[
             pltpu.VMEM((2, layers_held, block_rows, CHUNK), kind),
             pltpu.VMEM((2, 3, block_rows, CHUNK), kind),
@@ -517,8 +513,6 @@
             pltpu.VMEM((2, 2, tok_rows, CHUNK), jnp.float32),
             pltpu.VMEM((chunks, 2, tok_rows, CHUNK), jnp.float32),
             pltpu.VMEM((2, tok_rows, CHUNK), jnp.float32),
-            pltpu.VMEM((2, 2, tok_rows, CHUNK), kind),
-            pltpu.VMEM((2, 2, rows, CHUNK), kind),
             dma((2,)),
             dma((2, 3)),
             dma((steps, 3)),
@@ -536,13 +530,22 @@
             dma((2,)),
             dma((2, 2)),
             dma((chunks, 2)),
-            dma((2, 2)),
-            dma((2,)),
         ],
         compiler_params=pltpu.CompilerParams(
-            collective_id=0, has_side_effects=True, vmem_limit_bytes=60 * 2**20
+            collective_id=0, has_side_effects=True, vmem_limit_bytes=52 * 2**20
         ),
-    )(old_pieces, section_inputs, old_sec, new_sec, old_ord, new_ord, freq)
+    )(old_pieces, section_inputs, old_sec, new_sec, old_ord.T, new_ord.T, freq)
+    shard, kv = pl.pallas_call(
+        store_kernel,
+        out_shape=(
+            jax.ShapeDtypeStruct((2, rows, kv_width), kind),
+            jax.ShapeDtypeStruct((1, tok_rows, 2 * kv_width), kind),
+        ),
+        in_specs=[vmem, vmem],
+        out_specs=(hbm, hbm),
+        scratch_shapes=[dma((chunks,)), dma((2, chunks))],
+        compiler_params=pltpu.CompilerParams(vmem_limit_bytes=2**20),
+    )(held_shard, held_kv)
     return shard.reshape(1, 2 * rows, kv_width), kv
 
 

time: 405 us -> 397 us (0.980)
  local copies, waits for them, and re-layouts: 11.9 us -> 0 us
    unnamed x6 -> x0, local copies, waits for them, and re-layouts: 11.9 us -> none
    pallas_call x0 -> x1, Pallas kernels: none -> 4.11 us  [per_device_chain(): pl.pallas_call(store_kernel, out_shape=(jax.ShapeDtypeStruct((2, rows, kv...]
where the time goes in v1:
time: 397 us
  Pallas kernels  396 us (100%)
    pallas_call x1, Pallas kernels, per_device_chain(): pl.pallas_call(functools.partial(chain_kernel, block_rows, piece_rows), o...  392 us

profile of v1, /device:TPU:0, one launch (start us, length us, event | category | flops | bytes accessed | tf_op | source)
XLA Modules:
  0.0 396.9 jit_solution(15015490034667468979)
XLA Ops:
  0.6 392.2 %shard_map.86 = (bf16[8,2,2048,128]{3,2,1,0:T(8,128)(2,1)S(1)}, bf16[2,8,512,128]{3,2,1,0:T(8,128)(2,1)S(1)}, bf16[8,2,2048,128]{3,2,1,0:T(8,128)(2,1)}, bf16[8,2,2048,128]{3,2,1,0:T(8,128)(2,1)}) custom-call(bf16[1,2,2048,1024]{3,2,1,0:T(8,128)(2,1)} %old_ref.1, bf16[1,512,8192]{2,1,0:T(8,128)(2,1)} %tok_ref.1, s32[8]{0:T(128)} %old_sec.1, s32[8]{0:T(128)} %new_sec.1, ...), custom_call_target="tpu_custom_call" | custom-call | tf_op jit(solution)/shard_map/pallas_call | solution.py:490
  392.8 4.1 %shard_map.87 = (bf16[2,2048,1024]{2,1,0:T(8,128)(2,1)}, bf16[1,512,2048]{2,1,0:T(8,128)(2,1)}) custom-call(bf16[8,2,2048,128]{3,2,1,0:T(8,128)(2,1)S(1)} %get-tuple-element.6.held_shard, bf16[2,8,512,128]{3,2,1,0:T(8,128)(2,1)S(1)} %get-tuple-element.7.held_kv), custom_call_target="tpu_custom_call" | custom-call | tf_op jit(solution)/shard_map/pallas_call | solution.py:538

commit v2 on v1

--- a/solution.py
+++ b/solution.py
@@ -19,6 +19,8 @@
 RETURN_LAG = 6
 CHUNK_STEPS = 3
 PIECES_PER_STEP = 3
+RAW_BLOCKS = 3
+RAW_START = 12
 
 
 def chain_kernel(
@@ -26,10 +28,12 @@
     old_ref, tok_ref, old_sec, new_sec, old_ord, new_ord, freq_ref,
     shard_ref, kv_ref, relay_ref, middle_ref,
     oldv, send, keep, recv, held, forv, cross, tokv, cos_t, sin_t,
-    relay_w, middle_w, sums, sumr, acc,
+    relay_w, middle_w, sums, sumr, acc, raw, raw_send, raw_own, raw_foreign,
     old_sem, sec_send_sem, sec_recv_sem, x_send_sem, x_recv_sem, own_send_sem, relay_sem,
     middle_sem, fwd_send_sem, ret_send_sem, cross_sem, tok_sem, piece_send_sem, piece_recv_sem,
     weight_sem, sum_send_sem, sum_recv_sem,
+    raw_send_sem, raw_recv_sem, raw_sec_send_sem, raw_sec_recv_sem, raw_x_send_sem, raw_x_recv_sem,
+    raw_own_sem,
 ):
     rows = old_ref.shape[2]
     kv_width = old_ref.shape[3]
@@ -38,6 +42,7 @@
     chunks = kv_width // CHUNK
     blocks = rows // block_rows
     steps = chunks * blocks
+    early = steps - RAW_BLOCKS
     pieces = tok_rows // piece_rows
     layers = old_sec.shape[0]
 
@@ -160,6 +165,42 @@
             device_id_type=MESH,
         )
 
+    def raw_copy(u):
+        j, at = place_of(early + u)
+        return pltpu.make_async_remote_copy(
+            src_ref=old_ref.at[0, :, at, pl.ds(j * CHUNK, CHUNK)],
+            dst_ref=raw.at[u],
+            send_sem=raw_send_sem.at[u],
+            recv_sem=raw_recv_sem.at[u],
+            device_id=across,
+            device_id_type=MESH,
+        )
+
+    def raw_sec_copy(u, offset):
+        return pltpu.make_async_remote_copy(
+            src_ref=raw_send.at[offset - 1],
+            dst_ref=recv.at[u, offset - 1],
+            send_sem=raw_sec_send_sem.at[offset - 1],
+            recv_sem=raw_sec_recv_sem.at[u, offset - 1],
+            device_id={"section": section_at(offset)},
+            device_id_type=MESH,
+        )
+
+    def raw_x_copy(u):
+        j, at = place_of(early + u)
+        return pltpu.make_async_remote_copy(
+            src_ref=raw_foreign,
+            dst_ref=middle_ref.at[j, x, at],
+            send_sem=raw_x_send_sem,
+            recv_sem=raw_x_recv_sem.at[u],
+            device_id=partner,
+            device_id_type=MESH,
+        )
+
+    def raw_own_copy(u):
+        j, at = place_of(early + u)
+        return pltpu.make_async_copy(raw_own, middle_ref.at[j, x, at], raw_own_sem)
+
     def piece_copy(p):
         at = pl.ds(pl.multiple_of(p * piece_rows, piece_rows), piece_rows)
         column = (1 - side) * half_width
@@ -189,6 +230,11 @@
             weight_sem.at[which],
         )
 
+    @pl.when(inner)
+    def _():
+        for u in range(RAW_BLOCKS):
+            raw_copy(u).start()
+
     tile = min(256, tok_rows)
     tiles = tok_rows // tile
 
@@ -324,7 +370,7 @@
             low, high = oldv[t % 2, 0], oldv[t % 2, 1]
             for offset in (2, 3, 1):
                 send[t % 2, offset - 1] = jnp.where(target_low == section_at(offset), low, high)
-            keep[t % 4] = jnp.where(target_low == sec, low, high)
+            keep[t % 3] = jnp.where(target_low == sec, low, high)
             for offset in (2, 3, 1):
                 sec_copy(t, offset).start()
 
@@ -352,7 +398,7 @@
                 x_copy(t - 2).wait_send()
 
             j, at = place_of(t)
-            own, foreign = keep[t % 4], keep[t % 4]
+            own, foreign = keep[t % 3], keep[t % 3]
             for offset in (1, 2, 3):
                 arrived = recv[t, offset - 1]
                 own = jnp.where(own_from == section_at(offset), arrived, own)
@@ -370,14 +416,57 @@
             def _():
                 own_copy(t, False).start()
 
-            @pl.when(inner)
+            @pl.when(inner & (t < early))
             def _():
                 own_copy(t, True).start()
 
+        since_raw = tau - RAW_START
+        u = since_raw // 2
+
+        @pl.when(inner & (since_raw >= 0) & (since_raw % 2 == 0) & (u < RAW_BLOCKS))
+        def _():
+            raw_copy(u).wait()
+
+            @pl.when(u >= 1)
+            def _():
+                for offset in (1, 2, 3):
+                    raw_sec_copy(u - 1, offset).wait_send()
+
+            low, high = raw[u, 0], raw[u, 1]
+            for offset in (2, 3, 1):
+                raw_send[offset - 1] = jnp.where(target_low == section_at(offset), low, high)
+            for offset in (2, 3, 1):
+                raw_sec_copy(u, offset).start()
+
+        @pl.when(inner & (since_raw >= 2) & (since_raw % 2 == 0) & (u < RAW_BLOCKS + 1))
+        def _():
+            last = u - 1
+            for offset in (1, 2, 3):
+                raw_sec_copy(last, offset).wait_recv()
+            kept = jnp.where(target_low == sec, raw[last, 0], raw[last, 1])
+            own, foreign = kept, kept
+            for offset in (1, 2, 3):
+                arrived = recv[last, offset - 1]
+                own = jnp.where(own_from == section_at(offset), arrived, own)
+                foreign = jnp.where(foreign_from == section_at(offset), arrived, foreign)
+            raw_foreign[...] = foreign
+            raw_own[...] = own
+            raw_x_copy(last).start()
+            raw_own_copy(last).start()
+
+        @pl.when(inner & (since_raw >= 3) & (since_raw % 2 == 1) & (u < RAW_BLOCKS + 1))
+        def _():
+            raw_own_copy(u - 1).wait()
+            raw_x_copy(u - 1).wait()
+
         @pl.when(inner & (tau >= RETURN_LAG) & (tau < steps + RETURN_LAG))
         def _():
             t = tau - RETURN_LAG
-            own_copy(t, True).wait_recv()
+
+            @pl.when(t < early)
+            def _():
+                own_copy(t, True).wait_recv()
+
             cross_copy(t, False).start()
 
         @pl.when(inner & (tau >= CROSS_LAG) & (tau < steps + CROSS_LAG))
@@ -417,14 +506,22 @@
             sec_copy(t, offset).wait_send()
         x_copy(t).wait_send()
 
+    @pl.when(inner)
+    def _():
+        for offset in (1, 2, 3):
+            raw_sec_copy(RAW_BLOCKS - 1, offset).wait_send()
+
     def drain(t, carry):
         @pl.when(outer)
         def _():
             own_copy(t, False).wait_send()
 
+        @pl.when(inner & (t < early))
+        def _():
+            own_copy(t, True).wait_send()
+
         @pl.when(inner)
         def _():
-            own_copy(t, True).wait_send()
             cross_copy(t, False).wait_send()
             cross_copy(t, True).wait_send()
 
@@ -500,7 +597,7 @@
         scratch_shapes=[
             pltpu.VMEM((2, layers_held, block_rows, CHUNK), kind),
             pltpu.VMEM((2, 3, block_rows, CHUNK), kind),
-            pltpu.VMEM((4, block_rows, CHUNK), kind),
+            pltpu.VMEM((3, block_rows, CHUNK), kind),
             pltpu.VMEM((steps, 3, block_rows, CHUNK), kind),
             pltpu.VMEM((chunks, 2, rows, CHUNK), kind),
             pltpu.VMEM((2, block_rows, CHUNK), kind),
@@ -513,6 +610,10 @@
             pltpu.VMEM((2, 2, tok_rows, CHUNK), jnp.float32),
             pltpu.VMEM((chunks, 2, tok_rows, CHUNK), jnp.float32),
             pltpu.VMEM((2, tok_rows, CHUNK), jnp.float32),
+            pltpu.VMEM((RAW_BLOCKS, layers_held, block_rows, CHUNK), kind),
+            pltpu.VMEM((3, block_rows, CHUNK), kind),
+            pltpu.VMEM((block_rows, CHUNK), kind),
+            pltpu.VMEM((block_rows, CHUNK), kind),
             dma((2,)),
             dma((2, 3)),
             dma((steps, 3)),
@@ -530,9 +631,16 @@
             dma((2,)),
             dma((2, 2)),
             dma((chunks, 2)),
+            dma((RAW_BLOCKS,)),
+            dma((RAW_BLOCKS,)),
+            dma((3,)),
+            dma((RAW_BLOCKS, 3)),
+            dma,
+            dma((RAW_BLOCKS,)),
+            dma,
         ],
         compiler_params=pltpu.CompilerParams(
-            collective_id=0, has_side_effects=True, vmem_limit_bytes=52 * 2**20
+            collective_id=0, has_side_effects=True, vmem_limit_bytes=107 * 2**19
         ),
     )(old_pieces, section_inputs, old_sec, new_sec, old_ord.T, new_ord.T, freq)
     shard, kv = pl.pallas_call(

time: 397 us -> 385 us (0.970)
  Pallas kernels: 396 us -> 384 us
    pallas_call x1, Pallas kernels: 392 us -> 380 us  [per_device_chain(): pl.pallas_call(functools.partial(chain_kernel, block_rows, piece_rows), o...]
where the time goes in v2:
time: 385 us; the launch traced here: 384 us
  Pallas kernels  384 us (100%)
    pallas_call x1, Pallas kernels, per_device_chain(): pl.pallas_call(functools.partial(chain_kernel, block_rows, piece_rows), o...  380 us

profile of v2, /device:TPU:0, one launch (start us, length us, event | category | flops | bytes accessed | tf_op | source)
XLA Modules:
  0.0 384.4 jit_solution(1112249061239134583)
XLA Ops:
  0.6 379.6 %shard_map.86 = (bf16[8,2,2048,128]{3,2,1,0:T(8,128)(2,1)S(1)}, bf16[2,8,512,128]{3,2,1,0:T(8,128)(2,1)S(1)}, bf16[8,2,2048,128]{3,2,1,0:T(8,128)(2,1)}, bf16[8,2,2048,128]{3,2,1,0:T(8,128)(2,1)}) custom-call(bf16[1,2,2048,1024]{3,2,1,0:T(8,128)(2,1)} %old_ref.1, bf16[1,512,8192]{2,1,0:T(8,128)(2,1)} %tok_ref.1, s32[8]{0:T(128)} %old_sec.1, s32[8]{0:T(128)} %new_sec.1, ...), custom_call_target="tpu_custom_call" | custom-call | tf_op jit(solution)/shard_map/pallas_call | solution.py:587
  380.3 4.1 %shard_map.87 = (bf16[2,2048,1024]{2,1,0:T(8,128)(2,1)}, bf16[1,512,2048]{2,1,0:T(8,128)(2,1)}) custom-call(bf16[8,2,2048,128]{3,2,1,0:T(8,128)(2,1)S(1)} %get-tuple-element.6.held_shard, bf16[2,8,512,128]{3,2,1,0:T(8,128)(2,1)S(1)} %get-tuple-element.7.held_kv), custom_call_target="tpu_custom_call" | custom-call | tf_op jit(solution)/shard_map/pallas_call | solution.py:646

commit v3 on v2

--- a/solution.py
+++ b/solution.py
@@ -19,21 +19,23 @@
 RETURN_LAG = 6
 CHUNK_STEPS = 3
 PIECES_PER_STEP = 3
-RAW_BLOCKS = 3
+RAW_BLOCKS = 4
 RAW_START = 12
+SUM_PIECES = 4
 
 
 def chain_kernel(
     block_rows, piece_rows,
-    old_ref, tok_ref, old_sec, new_sec, old_ord, new_ord, freq_ref,
+    old_ref, tok_ref, old_sec_ref, new_sec_ref, old_ord_ref, new_ord_ref, freq_hbm,
     shard_ref, kv_ref, relay_ref, middle_ref,
+    old_sec, new_sec, old_ord, new_ord, freq_ref,
     oldv, send, keep, recv, held, forv, cross, tokv, cos_t, sin_t,
-    relay_w, middle_w, sums, sumr, acc, raw, raw_send, raw_own, raw_foreign,
+    relay_w, middle_w, sums, sumr, acc, raw_send, raw_own, raw_foreign,
     old_sem, sec_send_sem, sec_recv_sem, x_send_sem, x_recv_sem, own_send_sem, relay_sem,
     middle_sem, fwd_send_sem, ret_send_sem, cross_sem, tok_sem, piece_send_sem, piece_recv_sem,
     weight_sem, sum_send_sem, sum_recv_sem,
     raw_send_sem, raw_recv_sem, raw_sec_send_sem, raw_sec_recv_sem, raw_x_send_sem, raw_x_recv_sem,
-    raw_own_sem,
+    raw_own_sem, table_sem,
 ):
     rows = old_ref.shape[2]
     kv_width = old_ref.shape[3]
@@ -43,8 +45,11 @@
     blocks = rows // block_rows
     steps = chunks * blocks
     early = steps - RAW_BLOCKS
+    pairs = steps // 2
+    chunk_pairs = blocks // 2
+    part_rows = tok_rows // SUM_PIECES
     pieces = tok_rows // piece_rows
-    layers = old_sec.shape[0]
+    layers = old_sec_ref.shape[0]
 
     sec = lax.axis_index("section")
     member = lax.axis_index("fsdp")
@@ -90,11 +95,27 @@
             tok_ref.at[0, :, pl.ds(column, half_width)], tokv.at[which], tok_sem.at[which]
         )
 
+    tables = [
+        pltpu.make_async_copy(source, target, table_sem.at[i])
+        for i, (source, target) in enumerate(
+            (
+                (old_sec_ref, old_sec),
+                (new_sec_ref, new_sec),
+                (old_ord_ref, old_ord),
+                (new_ord_ref, new_ord),
+                (freq_hbm, freq_ref),
+            )
+        )
+    ]
+    for table in tables:
+        table.start()
     old_load(0).start()
     old_load(1).start()
     tok_load(0).start()
     tok_load(1).start()
 
+    for table in tables:
+        table.wait()
     target_low = jnp.int32(0)
     own_from, foreign_from = jnp.int32(0), jnp.int32(0)
     old_first, new_first = jnp.int32(0), jnp.int32(0)
@@ -122,6 +143,10 @@
     def place_of(t):
         return t // blocks, pl.ds(pl.multiple_of((t % blocks) * block_rows, block_rows), block_rows)
 
+    def pair_of(p):
+        first = pl.multiple_of((p % chunk_pairs) * 2 * block_rows, 2 * block_rows)
+        return p // chunk_pairs, pl.ds(first, 2 * block_rows)
+
     def sec_copy(t, offset):
         return pltpu.make_async_remote_copy(
             src_ref=send.at[t % 2, offset - 1],
@@ -143,24 +168,24 @@
             device_id_type=MESH,
         )
 
-    def own_copy(t, to_middle):
-        j, at = place_of(t)
+    def own_copy(p, to_middle):
+        j, at = pair_of(p)
         return pltpu.make_async_remote_copy(
             src_ref=held.at[j, :, at],
             dst_ref=(middle_ref if to_middle else relay_ref).at[j, :, at],
-            send_sem=own_send_sem.at[t],
-            recv_sem=(middle_sem if to_middle else relay_sem).at[t],
+            send_sem=own_send_sem.at[p],
+            recv_sem=(middle_sem if to_middle else relay_sem).at[p],
             device_id=across if to_middle else beside,
             device_id_type=MESH,
         )
 
-    def cross_copy(t, forward):
-        j, at = place_of(t)
+    def cross_copy(p, forward):
+        j, at = pair_of(p)
         return pltpu.make_async_remote_copy(
             src_ref=(relay_ref if forward else middle_ref).at[j, :, at],
             dst_ref=cross.at[j, :, at],
-            send_sem=(fwd_send_sem if forward else ret_send_sem).at[t],
-            recv_sem=cross_sem.at[t],
+            send_sem=(fwd_send_sem if forward else ret_send_sem).at[p],
+            recv_sem=cross_sem.at[p],
             device_id=across if forward else beside,
             device_id_type=MESH,
         )
@@ -169,7 +194,7 @@
         j, at = place_of(early + u)
         return pltpu.make_async_remote_copy(
             src_ref=old_ref.at[0, :, at, pl.ds(j * CHUNK, CHUNK)],
-            dst_ref=raw.at[u],
+            dst_ref=recv.at[early + u, pl.ds(0, old_ref.shape[1])],
             send_sem=raw_send_sem.at[u],
             recv_sem=raw_recv_sem.at[u],
             device_id=across,
@@ -213,12 +238,15 @@
             device_id_type=MESH,
         )
 
-    def sum_copy(j, which):
+    def part_of(q):
+        return pl.ds(pl.multiple_of(q * part_rows, part_rows), part_rows)
+
+    def sum_copy(j, which, q):
         return pltpu.make_async_remote_copy(
-            src_ref=sums.at[j % 2, which],
-            dst_ref=sumr.at[j, which],
-            send_sem=sum_send_sem.at[j % 2, which],
-            recv_sem=sum_recv_sem.at[j, which],
+            src_ref=sums.at[j % 2, which, part_of(q)],
+            dst_ref=sumr.at[j, which, part_of(q)],
+            send_sem=sum_send_sem.at[j % 2, which, q],
+            recv_sem=sum_recv_sem.at[j, which, q],
             device_id=beside,
             device_id_type=MESH,
         )
@@ -246,6 +274,27 @@
             tokv[which, at, pl.ds(rows, rows)], weights[1], preferred_element_type=jnp.float32
         )
         return near + far
+
+    def half_product(which, weights, at, half):
+        count = rows // 2
+        near = jnp.dot(
+            tokv[which, at, pl.ds(half * count, count)],
+            weights[0, pl.ds(half * count, count)],
+            preferred_element_type=jnp.float32,
+        )
+        far = jnp.dot(
+            tokv[which, at, pl.ds(rows + half * count, count)],
+            weights[1, pl.ds(half * count, count)],
+            preferred_element_type=jnp.float32,
+        )
+        return near + far
+
+    def each_part(body):
+        def run(q, carry):
+            body(q)
+            return carry
+
+        lax.fori_loop(0, SUM_PIECES, run, 0)
 
     def each_tile(body):
         def run(i, carry):
@@ -290,13 +339,13 @@
         def _():
             @pl.when(j >= 2)
             def _():
-                sum_copy(j - 2, 0).wait_send()
-
-            def foreign(at):
-                sums[j % 2, 0, at] = product(2, held.at[j], at)
-
-            each_tile(foreign)
-            sum_copy(j, 0).start()
+                each_part(lambda q: sum_copy(j - 2, 0, q).wait_send())
+
+            def foreign(q):
+                sums[j % 2, 0, part_of(q)] = product(2, held.at[j], part_of(q))
+                sum_copy(j, 0, q).start()
+
+            each_part(foreign)
             weight_load(j, 0).wait()
             weight_load(j, 1).wait()
 
@@ -314,20 +363,31 @@
             each_tile(mine)
 
     def compute_cross(j):
-        for b in range(blocks):
-            cross_copy(j * blocks + b, True).wait_recv()
+        first, second = j * chunk_pairs, j * chunk_pairs + 1
+        ahead = inner & (sec % 2 == 0) & (j == chunks - 1)
+
+        @pl.when(jnp.logical_not(ahead))
+        def _():
+            cross_copy(first, True).wait_recv()
 
         @pl.when(inner)
         def _():
             @pl.when(j >= 2)
             def _():
-                sum_copy(j - 2, 1).wait_send()
-
-            def foreign(at):
-                sums[j % 2, 1, at] = product(2, cross.at[j], at)
-
-            each_tile(foreign)
-            sum_copy(j, 1).start()
+                each_part(lambda q: sum_copy(j - 2, 1, q).wait_send())
+
+            def early_part(at):
+                sums[j % 2, 1, at] = half_product(2, cross.at[j], at, 0)
+
+            each_tile(early_part)
+            cross_copy(second, True).wait_recv()
+
+            def late_part(q):
+                at = part_of(q)
+                sums[j % 2, 1, at] = sums[j % 2, 1, at] + half_product(2, cross.at[j], at, 1)
+                sum_copy(j, 1, q).start()
+
+            each_part(late_part)
 
             def mine(at):
                 acc[1, at] = acc[1, at] + product(0, cross.at[j], at)
@@ -336,25 +396,34 @@
 
         @pl.when(outer)
         def _():
+            cross_copy(second, True).wait_recv()
+
             def mine(at):
                 acc[1, at] = product(0, cross.at[j], at)
 
             each_tile(mine)
 
-        shard_ref[j] = jnp.where(flipped, cross[j], held[j])
-
-        @pl.when(outer)
-        def _():
-            for which in range(2):
-                sum_copy(j, which).wait_recv()
-                acc[which] = acc[which] + sumr[j, which]
-
-        first, second = acc[0], acc[1]
-        keys = jnp.where(own_is_key, first, second)
-        values = jnp.where(own_is_key, second, first)
-        turned = keys * cos_t[...] + pltpu.roll(keys, CHUNK // 2, 1) * sin_t[...]
-        kv_ref[0, j] = turned.astype(kv_ref.dtype)
-        kv_ref[1, j] = values.astype(kv_ref.dtype)
+        columns = pl.ds(pl.multiple_of(j * CHUNK, CHUNK), CHUNK)
+        shard_ref[:, :, columns] = jnp.where(flipped, cross[j], held[j])
+        value_columns = pl.ds(pl.multiple_of(kv_width + j * CHUNK, CHUNK), CHUNK)
+
+        def finish(q):
+            at = part_of(q)
+
+            @pl.when(outer)
+            def _():
+                for which in range(2):
+                    sum_copy(j, which, q).wait_recv()
+                    acc[which, at] = acc[which, at] + sumr[j, which, at]
+
+            lower, higher = acc[0, at], acc[1, at]
+            keys = jnp.where(own_is_key, lower, higher)
+            values = jnp.where(own_is_key, higher, lower)
+            turned = keys * cos_t[at] + pltpu.roll(keys, CHUNK // 2, 1) * sin_t[at]
+            kv_ref[at, columns] = turned.astype(kv_ref.dtype)
+            kv_ref[at, value_columns] = values.astype(kv_ref.dtype)
+
+        each_part(finish)
 
     def step(tau, carry):
         @pl.when(tau < steps)
@@ -412,13 +481,13 @@
             t = tau - 3
             x_copy(t).wait_recv()
 
-            @pl.when(outer)
-            def _():
-                own_copy(t, False).start()
-
-            @pl.when(inner & (t < early))
-            def _():
-                own_copy(t, True).start()
+            @pl.when(outer & (t % 2 == 1))
+            def _():
+                own_copy(t // 2, False).start()
+
+            @pl.when(inner & (t % 2 == 1) & (t < early))
+            def _():
+                own_copy(t // 2, True).start()
 
         since_raw = tau - RAW_START
         u = since_raw // 2
@@ -432,7 +501,7 @@
                 for offset in (1, 2, 3):
                     raw_sec_copy(u - 1, offset).wait_send()
 
-            low, high = raw[u, 0], raw[u, 1]
+            low, high = recv[early + u, 0], recv[early + u, 1]
             for offset in (2, 3, 1):
                 raw_send[offset - 1] = jnp.where(target_low == section_at(offset), low, high)
             for offset in (2, 3, 1):
@@ -443,7 +512,7 @@
             last = u - 1
             for offset in (1, 2, 3):
                 raw_sec_copy(last, offset).wait_recv()
-            kept = jnp.where(target_low == sec, raw[last, 0], raw[last, 1])
+            kept = jnp.where(target_low == sec, recv[early + last, 0], recv[early + last, 1])
             own, foreign = kept, kept
             for offset in (1, 2, 3):
                 arrived = recv[last, offset - 1]
@@ -459,21 +528,28 @@
             raw_own_copy(u - 1).wait()
             raw_x_copy(u - 1).wait()
 
-        @pl.when(inner & (tau >= RETURN_LAG) & (tau < steps + RETURN_LAG))
-        def _():
-            t = tau - RETURN_LAG
-
-            @pl.when(t < early)
-            def _():
-                own_copy(t, True).wait_recv()
-
-            cross_copy(t, False).start()
-
-        @pl.when(inner & (tau >= CROSS_LAG) & (tau < steps + CROSS_LAG))
-        def _():
-            t = tau - CROSS_LAG
-            own_copy(t, False).wait_recv()
-            cross_copy(t, True).start()
+        back = tau - RETURN_LAG
+
+        @pl.when(inner & (back >= 0) & (back < steps) & (back % 2 == 1))
+        def _():
+            @pl.when(back < early)
+            def _():
+                own_copy(back // 2, True).wait_recv()
+
+            cross_copy(back // 2, False).start()
+
+        forth = tau - CROSS_LAG
+
+        @pl.when(inner & (forth >= 0) & (forth < steps) & (forth % 2 == 1))
+        def _():
+            p = forth // 2
+            own_copy(p, False).wait_recv()
+
+            @pl.when((sec % 2 == 0) & (p == pairs - 1))
+            def _():
+                cross_copy(p - 1, True).wait_recv()
+
+            cross_copy(p, True).start()
 
         @pl.when(tau == 4)
         def _():
@@ -511,23 +587,23 @@
         for offset in (1, 2, 3):
             raw_sec_copy(RAW_BLOCKS - 1, offset).wait_send()
 
-    def drain(t, carry):
+    def drain(p, carry):
         @pl.when(outer)
         def _():
-            own_copy(t, False).wait_send()
-
-        @pl.when(inner & (t < early))
-        def _():
-            own_copy(t, True).wait_send()
+            own_copy(p, False).wait_send()
+
+        @pl.when(inner & (2 * p < early))
+        def _():
+            own_copy(p, True).wait_send()
 
         @pl.when(inner)
         def _():
-            cross_copy(t, False).wait_send()
-            cross_copy(t, True).wait_send()
+            cross_copy(p, False).wait_send()
+            cross_copy(p, True).wait_send()
 
         return carry
 
-    lax.fori_loop(0, steps, drain, 0)
+    lax.fori_loop(0, pairs, drain, 0)
 
     @pl.when(outer)
     def _():
@@ -541,23 +617,19 @@
         @pl.when(inner)
         def _():
             for which in range(2):
-                sum_copy(j, which).wait_send()
+                each_part(lambda q: sum_copy(j, which, q).wait_send())
 
 
 def store_kernel(held_shard, held_kv, shard_ref, kv_ref, shard_sem, kv_sem):
-    chunks = held_shard.shape[0]
-    kv_width = shard_ref.shape[2]
-    copies = []
-    for j in range(chunks):
-        at = pl.ds(j * CHUNK, CHUNK)
-        copies.append(
-            pltpu.make_async_copy(held_shard.at[j], shard_ref.at[:, :, at], shard_sem.at[j])
-        )
-        for which in range(2):
-            at = pl.ds(which * kv_width + j * CHUNK, CHUNK)
+    halves, rows = held_shard.shape[:2]
+    cuts = shard_sem.shape[1]
+    copies = [pltpu.make_async_copy(held_kv, kv_ref.at[0], kv_sem)]
+    for half in range(halves):
+        for cut in range(cuts):
+            at = pl.ds(cut * (rows // cuts), rows // cuts)
             copies.append(
                 pltpu.make_async_copy(
-                    held_kv.at[which, j], kv_ref.at[0, :, at], kv_sem.at[which, j]
+                    held_shard.at[half, at], shard_ref.at[half, at], shard_sem.at[half, cut]
                 )
             )
     for copy in copies:
@@ -582,19 +654,23 @@
     kind = old_pieces.dtype
     dma = pltpu.SemaphoreType.DMA
     hbm = pl.BlockSpec(memory_space=pltpu.HBM)
-    smem = pl.BlockSpec(memory_space=pltpu.SMEM)
     vmem = pl.BlockSpec(memory_space=pltpu.VMEM)
     held_shard, held_kv, _, _ = pl.pallas_call(
         functools.partial(chain_kernel, block_rows, piece_rows),
         out_shape=(
-            pltpu.VMEM((chunks, 2, rows, CHUNK), kind),
-            pltpu.VMEM((2, chunks, tok_rows, CHUNK), kind),
+            pltpu.VMEM((2, rows, kv_width), kind),
+            pltpu.VMEM((tok_rows, 2 * kv_width), kind),
             jax.ShapeDtypeStruct((chunks, 2, rows, CHUNK), kind),
             jax.ShapeDtypeStruct((chunks, 2, rows, CHUNK), kind),
         ),
-        in_specs=[hbm, hbm, smem, smem, smem, smem, vmem],
+        in_specs=[hbm] * 7,
         out_specs=(vmem, vmem, hbm, hbm),
         scratch_shapes=[
+            pltpu.SMEM(old_sec.shape, jnp.int32),
+            pltpu.SMEM(new_sec.shape, jnp.int32),
+            pltpu.SMEM(old_ord.shape[::-1], jnp.int32),
+            pltpu.SMEM(new_ord.shape[::-1], jnp.int32),
+            pltpu.VMEM(freq.shape, jnp.float32),
             pltpu.VMEM((2, layers_held, block_rows, CHUNK), kind),
             pltpu.VMEM((2, 3, block_rows, CHUNK), kind),
             pltpu.VMEM((3, block_rows, CHUNK), kind),
@@ -610,7 +686,6 @@
             pltpu.VMEM((2, 2, tok_rows, CHUNK), jnp.float32),
             pltpu.VMEM((chunks, 2, tok_rows, CHUNK), jnp.float32),
             pltpu.VMEM((2, tok_rows, CHUNK), jnp.float32),
-            pltpu.VMEM((RAW_BLOCKS, layers_held, block_rows, CHUNK), kind),
             pltpu.VMEM((3, block_rows, CHUNK), kind),
             pltpu.VMEM((block_rows, CHUNK), kind),
             pltpu.VMEM((block_rows, CHUNK), kind),
@@ -619,18 +694,18 @@
             dma((steps, 3)),
             dma((2,)),
             dma((steps,)),
-            dma((steps,)),
-            dma((steps,)),
-            dma((steps,)),
-            dma((steps,)),
-            dma((steps,)),
-            dma((steps,)),
+            dma((steps // 2,)),
+            dma((steps // 2,)),
+            dma((steps // 2,)),
+            dma((steps // 2,)),
+            dma((steps // 2,)),
+            dma((steps // 2,)),
             dma((2,)),
             dma((pieces,)),
             dma((pieces,)),
             dma((2,)),
-            dma((2, 2)),
-            dma((chunks, 2)),
+            dma((2, 2, SUM_PIECES)),
+            dma((chunks, 2, SUM_PIECES)),
             dma((RAW_BLOCKS,)),
             dma((RAW_BLOCKS,)),
             dma((3,)),
@@ -638,6 +713,7 @@
             dma,
             dma((RAW_BLOCKS,)),
             dma,
+            dma((5,)),
         ],
         compiler_params=pltpu.CompilerParams(
             collective_id=0, has_side_effects=True, vmem_limit_bytes=107 * 2**19
@@ -651,7 +727,7 @@
         ),
         in_specs=[vmem, vmem],
         out_specs=(hbm, hbm),
-        scratch_shapes=[dma((chunks,)), dma((2, chunks))],
+        scratch_shapes=[dma((2, 4)), dma],
         compiler_params=pltpu.CompilerParams(vmem_limit_bytes=2**20),
     )(held_shard, held_kv)
     return shard.reshape(1, 2 * rows, kv_width), kv

time: 385 us -> 381 us (0.990)
  Pallas kernels: 384 us -> 380 us
    pallas_call x1, Pallas kernels: 380 us -> 376 us  [per_device_chain(): pl.pallas_call(functools.partial(chain_kernel, block_rows, piece_rows), o...]
where the time goes in v3:
time: 381 us; the launch traced here: 380 us
  Pallas kernels  380 us (100%)
    pallas_call x1, Pallas kernels, per_device_chain(): pl.pallas_call(functools.partial(chain_kernel, block_rows, piece_rows), o...  376 us

profile of v3, /device:TPU:0, one launch (start us, length us, event | category | flops | bytes accessed | tf_op | source)
XLA Modules:
  0.0 380.4 jit_solution(2666390277759734892)
XLA Ops:
  0.6 375.8 %shard_map.86 = (bf16[2,2048,1024]{2,1,0:T(8,128)(2,1)S(1)}, bf16[512,2048]{1,0:T(8,128)(2,1)S(1)}, bf16[8,2,2048,128]{3,2,1,0:T(8,128)(2,1)}, bf16[8,2,2048,128]{3,2,1,0:T(8,128)(2,1)}) custom-call(bf16[1,2,2048,1024]{3,2,1,0:T(8,128)(2,1)} %old_ref.1, bf16[1,512,8192]{2,1,0:T(8,128)(2,1)} %tok_ref.1, s32[8]{0:T(128)} %old_sec_ref.1, s32[8]{0:T(128)} %new_sec_ref.1, ...), custom_call_target="tpu_custom_call" | custom-call | tf_op jit(solution)/shard_map/pallas_call | solution.py:658
  376.4 4.0 %shard_map.87 = (bf16[2,2048,1024]{2,1,0:T(8,128)(2,1)}, bf16[1,512,2048]{2,1,0:T(8,128)(2,1)}) custom-call(bf16[2,2048,1024]{2,1,0:T(8,128)(2,1)S(1)} %get-tuple-element.6.held_shard, bf16[512,2048]{1,0:T(8,128)(2,1)S(1)} %get-tuple-element.7.held_kv), custom_call_target="tpu_custom_call" | custom-call | tf_op jit(solution)/shard_map/pallas_call | solution.py:722
